TPU v7x, 32 devices: a whole 2x2x4 slice. The times are simulated.
32 devices in a mesh: groups: 2 (over y), ep: 16 (over z, x, core).
Axes of the slice: x: 2, y: 2, z: 4, core: 2. Of those that a mesh axis runs over, the one named last changes fastest.
Arguments:
- tokens: bfloat16 [512, 2880], P(('groups', 'ep')), parts along dimension 0, may hold values from -6 to 6
- routes: int32 [512, 4], P(('groups', 'ep')), parts along dimension 0, may hold values from 0 to 7, all different within a row; in each aligned block of 16 rows (0 to 15, 16 to 31, ...) at most 16 rows name the same one
- gate_fixed: int32 [512, 4], P(('groups', 'ep')), parts along dimension 0, may hold values from 1 to 65535
- gate_weight: bfloat16 [16, 2880, 720], P('ep'), may hold values from -0.109375 to 0.109375
- up_weight: bfloat16 [16, 2880, 720], P('ep'), may hold values from -0.109375 to 0.109375
- down_weight: bfloat16 [16, 720, 2880], P('ep'), may hold values from -0.15625 to 0.15625
Outputs:
- mixed: bfloat16 [512, 2880], P(('groups', 'ep')), parts along dimension 0
There are 2 independent parts, one for each index of `groups`. A program takes and returns all parts, laid end to end along the dimension named above; an argument that names none is the same for every part. Nothing has to cross between parts.
Inputs may be any that keep to these rules, and one draw needn't show every extreme that they name: `routes`: each row names 4 different experts; the 16 rows of one device name any one expert at most 16 times.
All inputs are finite; a program needn't handle non-finite values.
Results may differ from a plain program's by a relative error of at most 0.0065.
Values may be sent and summed in bfloat16 or wider, within the bound.
A program may use at most 64 MiB of HBM per device.

v0:
```python
import jax
import jax.numpy as jnp
from jax import lax
from jax.sharding import PartitionSpec as P


def swapped(value, axis, bit):
    mask = 2**bit
    pairs = [(source, source ^ mask) for source in range(lax.axis_size(axis))]
    return lax.ppermute(value, axis, pairs)


def expert_half(expert_rows, w_gate, w_up, w_down):
    gate_part = jnp.dot(expert_rows, w_gate, preferred_element_type=jnp.float32)
    up_part = jnp.dot(expert_rows, w_up, preferred_element_type=jnp.float32)
    hidden = (jax.nn.silu(gate_part) * up_part).astype(jnp.bfloat16)
    return jnp.dot(hidden, w_down, preferred_element_type=jnp.float32).astype(jnp.bfloat16)


def local(tokens, routes, gate_fixed, gate_weight, up_weight, down_weight):
    devices_ep = lax.axis_size("ep")
    experts = devices_ep // 2
    tok_count = tokens.shape[0]
    top_count = routes.shape[1]
    width = tokens.shape[1]
    capacity = 2 * tok_count * top_count // experts
    onehot = (routes[:, :, None] == jnp.arange(experts, dtype=jnp.int32)).astype(jnp.int32)
    flat_hot = onehot.reshape(tok_count * top_count, experts)
    before = jnp.cumsum(flat_hot, axis=0) - flat_hot
    position = jnp.sum(before * flat_hot, axis=1).reshape(tok_count, top_count)
    slot_index = routes * capacity + position
    select = (slot_index[:, :, None] == jnp.arange(experts * capacity, dtype=jnp.int32)).astype(
        jnp.int32
    )
    select = jnp.sum(select, axis=1).astype(jnp.bfloat16)
    packed = jnp.einsum("ts,td->sd", select, tokens, preferred_element_type=jnp.float32).astype(
        jnp.bfloat16
    )
    packed = packed.reshape(experts, 1, capacity, width)
    outgoing = jnp.broadcast_to(packed, (experts, 2, capacity, width)).reshape(
        devices_ep, capacity, width
    )
    received = lax.all_to_all(outgoing, "ep", split_axis=0, concat_axis=0, tiled=True)
    result = expert_half(received.reshape(-1, width), gate_weight[0], up_weight[0], down_weight[0])
    partial_value = result.reshape(received.shape[0], received.shape[1], width)
    parity = lax.axis_index("ep") % 2
    halves = partial_value.reshape(devices_ep, capacity, 2, width // 2)
    kept_half = lax.dynamic_index_in_dim(halves, parity, 2, keepdims=False)
    given_half = lax.dynamic_index_in_dim(halves, 1 - parity, 2, keepdims=False)
    partner = swapped(given_half, "ep", 0)
    reduced = (kept_half.astype(jnp.float32) + partner.astype(jnp.float32)).astype(jnp.bfloat16)
    returned = lax.all_to_all(reduced, "ep", split_axis=0, concat_axis=0, tiled=True)
    ordered = returned.reshape(experts, 2, capacity, width // 2).transpose(0, 2, 1, 3)
    expert_out = ordered.reshape(experts * capacity, width)
    picked = jnp.take(expert_out, slot_index.reshape(-1), axis=0).reshape(
        tok_count, top_count, width
    )
    weights = gate_fixed.astype(jnp.float32) / 65536.0
    mixed = jnp.sum(weights[:, :, None] * picked.astype(jnp.float32), axis=1)
    return mixed.astype(jnp.bfloat16)


def solution(mesh):
    placed = (
        P(("groups", "ep"), None),
        P(("groups", "ep"), None),
        P(("groups", "ep"), None),
        P("ep", None, None),
        P("ep", None, None),
        P("ep", None, None),
    )
    return jax.shard_map(
        local, mesh=mesh, in_specs=placed, out_specs=P(("groups", "ep"), None), check_vma=False
    )
```

profile of v0, /device:TPU:0, one launch (start us, length us, event | category | flops | bytes accessed | tf_op | source)
XLA Modules:
  0.0 96.8 jit_solution(15674971853271699350)
XLA Ops:
  0.0 0.8 copy.25
  1.0 0.1 reduce_window_sum.11
  1.1 0.2 select_reduce_fusion
  1.5 0.4 convolution_convert_fusion
  1.9 0.4 copy.28
  2.3 1.3 %broadcast_in_dim.24 = bf16[8,2,16,2880]{3,2,1,0:T(8,128)(2,1)} broadcast(bf16[8,16,2880]{2,1,0:T(8,128)(2,1)S(1)} %bitcast.38), dimensions={0,2,3} | broadcast | bytes 2211840 | tf_op jit(solution)/shard_map/broadcast_in_dim | solution.py:40
  3.6 7.4 %all-to-all-start = ((bf16[16,16,2880]{2,1,0:T(8,128)(2,1)}), bf16[16,16,2880]{2,1,0:T(8,128)(2,1)S(1)}, u32[]{:S(2)}, u32[]{:S(2)}) async-start(bf16[16,16,2880]{2,1,0:T(8,128)(2,1)} %bitcast.1), calls=%async_computation | async-start | bytes 3014656 | tf_op jit(solution)/shard_map/all_to_all | solution.py:43
  11.0 30.7 %all-to-all-done = bf16[16,16,2880]{2,1,0:T(8,128)(2,1)S(1)} async-done(((bf16[16,16,2880]{2,1,0:T(8,128)(2,1)}), bf16[16,16,2880]{2,1,0:T(8,128)(2,1)S(1)}, u32[]{:S(2)}, u32[]{:S(2)}) %all-to-all-start) | async-done | bytes 1474592 | tf_op jit(solution)/shard_map/all_to_all | solution.py:43
  41.7 3.5 %fusion.4 = f32[256,720]{0,1:T(8,128)S(1)} fusion(bf16[256,2880]{1,0:T(8,128)(2,1)S(1)} %bitcast.39, bf16[1,2880,720]{1,2,0:T(8,128)(2,1)} %param.9), kind=kOutput, calls=%fused_computation.5 | convolution fusion | flops 1061683200 | bytes 6359040 | tf_op jit(solution)/shard_map/dot_general | solution.py:14
  45.2 9.4 %fusion.6 = bf16[256,2880]{0,1:T(8,128)(2,1)} fusion(bf16[1,720,2880]{2,1,0:T(8,128)(2,1)} %param.11, bf16[256,2880]{1,0:T(8,128)(2,1)S(1)} %bitcast.40, bf16[1,2880,720]{1,2,0:T(8,128)(2,1)} %param.10, f32[256,720]{0,1:T(8,128)S(1)} %fusion.4), kind=kOutput, calls=%fused_computation.7 | convolution fusion | flops 2125209600 | bytes 11980800 | tf_op jit(solution)/shard_map/dot_general | solution.py:17
  54.6 1.8 %copy.29 = bf16[256,2880]{1,0:T(8,128)(2,1)S(1)} copy(bf16[256,2880]{0,1:T(8,128)(2,1)} %fusion.6) | data formatting | bytes 2949120 | tf_op jit(solution)/shard_map/convert_element_type | solution.py:17
  56.4 1.9 %reshape_reshape.3 = bf16[16,16,2,1440]{3,2,1,0:T(2,128)(2,1)S(1)} reshape(bf16[256,2880]{1,0:T(8,128)(2,1)S(1)} %copy.29) | data formatting | bytes 2949120 | tf_op jit(solution)/shard_map/reshape;reshape | solution.py:47
  58.4 3.6 %constant_dynamic-slice_fusion = (bf16[16,16,1,1440]{3,2,1,0:T(2,128)(2,1)S(1)}, f32[16,16,1,1440]{3,2,1,0:T(1,128)S(1)}) fusion(bf16[16,16,2,1440]{3,2,1,0:T(2,128)(2,1)S(1)} %reshape_reshape.3, s32[]{:T(128)S(6)} %select_n.39, s32[]{:T(128)S(6)} %select_n.38), kind=kLoop, calls=%fused_computation.30 | loop fusion | flops 368640 | bytes 3686408 | tf_op jit(solution)/shard_map/jit(dynamic_index_in_dim)/dynamic_slice | solution.py:49
  62.0 0.1 copy.36
  62.1 1.0 %collective-permute-start = (bf16[16,16,1440]{2,1,0:T(8,128)(2,1)S(1)}, bf16[16,16,1440]{2,1,0:T(8,128)(2,1)S(1)}, u32[]{:S(2)}, u32[]{:S(2)}) collective-permute-start(bf16[16,16,1440]{2,1,0:T(8,128)(2,1)S(1)} %bitcast.41), channel_id=1, source_target_pairs={{0,1},{1,0},{2,3},{3,2},{4,5},{5,4},{6,7},{7,6},{8,9},{9,8},{10,11... | collective-permute-start | bytes 2211848 | tf_op jit(solution)/shard_map/ppermute | solution.py:10
  63.2 1.9 %collective-permute-done = bf16[16,16,1440]{2,1,0:T(8,128)(2,1)S(1)} collective-permute-done((bf16[16,16,1440]{2,1,0:T(8,128)(2,1)S(1)}, bf16[16,16,1440]{2,1,0:T(8,128)(2,1)S(1)}, u32[]{:S(2)}, u32[]{:S(2)}) %collective-permute-start) | collective-permute-done | bytes 737312 | tf_op jit(solution)/shard_map/ppermute | solution.py:10
  65.1 1.1 %fusion.9 = bf16[16,16,1440]{2,1,0:T(8,128)(2,1)} fusion(f32[16,16,1,1440]{3,2,1,0:T(1,128)S(1)} %get-tuple-element.8, bf16[16,16,1440]{2,1,0:T(8,128)(2,1)S(1)} %collective-permute-done), kind=kLoop, calls=%fused_computation.10 | loop fusion | flops 1105920 | bytes 2949120 | tf_op jit(solution)/shard_map/convert_element_type | solution.py:51
  66.2 8.4 %all-to-all-start.1 = ((bf16[16,16,1440]{2,1,0:T(8,128)(2,1)}), bf16[16,16,1440]{2,1,0:T(8,128)(2,1)S(1)}, u32[]{:S(2)}, u32[]{:S(2)}) async-start(bf16[16,16,1440]{2,1,0:T(8,128)(2,1)} %fusion.9), calls=%async_computation.1 | async-start | bytes 1572864 | tf_op jit(solution)/shard_map/all_to_all | solution.py:52
  74.8 18.5 %all-to-all-done.1 = bf16[16,16,1440]{2,1,0:T(8,128)(2,1)S(1)} async-done(((bf16[16,16,1440]{2,1,0:T(8,128)(2,1)}), bf16[16,16,1440]{2,1,0:T(8,128)(2,1)S(1)}, u32[]{:S(2)}, u32[]{:S(2)}) %all-to-all-start.1) | async-done | bytes 737312 | tf_op jit(solution)/shard_map/all_to_all | solution.py:52
  93.3 0.8 copy.37
  94.1 0.6 reshape.72
  94.7 0.8 gather_fusion
  95.5 0.1 gather.7
  95.6 1.3 %multiply_reduce_fusion = bf16[16,2880]{1,0:T(8,128)(2,1)} fusion(bf16[16,4,2880]{2,1,0:T(4,128)(2,1)S(1)} %gather.7, f32[16,4]{1,0:T(8,128)S(1)} %copy.24, pred[16,4]{1,0:T(8,128)(4,1)S(1)} %get-tuple-element.5), kind=kLoop, calls=%fused_computation.16 | loop fusion | flops 691200 | bytes 461120 | tf_op jit(solution)/shard_map/reduce_sum | solution.py:59
  (15 shorter events, 0.6 us)
Async XLA Ops:
  0.0 1.5 %copy-start = (bf16[16,2880]{1,0:T(8,128)(2,1)S(1)}, bf16[16,2880]{1,0:T(8,128)(2,1)}, u32[]{:S(2)}) copy-start(bf16[16,2880]{1,0:T(8,128)(2,1)} %param.6) | copy-start | bytes 276484
  3.6 38.1 %all-to-all-start = ((bf16[16,16,2880]{2,1,0:T(8,128)(2,1)}), bf16[16,16,2880]{2,1,0:T(8,128)(2,1)S(1)}, u32[]{:S(2)}, u32[]{:S(2)}) async-start(bf16[16,16,2880]{2,1,0:T(8,128)(2,1)} %bitcast.1), calls=%async_computation | async-start | bytes 3014656 | tf_op jit(solution)/shard_map/all_to_all | solution.py:43
  62.1 3.0 %collective-permute-start = (bf16[16,16,1440]{2,1,0:T(8,128)(2,1)S(1)}, bf16[16,16,1440]{2,1,0:T(8,128)(2,1)S(1)}, u32[]{:S(2)}, u32[]{:S(2)}) collective-permute-start(bf16[16,16,1440]{2,1,0:T(8,128)(2,1)S(1)} %bitcast.41), channel_id=1, source_target_pairs={{0,1},{1,0},{2,3},{3,2},{4,5},{5,4},{6,7},{7,6},{8,9},{9,8},{10,11... | collective-permute-start | bytes 2211848 | tf_op jit(solution)/shard_map/ppermute | solution.py:10
  66.2 8.5 %copy-start.1 = (s32[16,4]{0,1:T(4,128)S(1)}, s32[16,4]{0,1:T(4,128)}, u32[]{:S(2)}) copy-start(s32[16,4]{0,1:T(4,128)} %param.8) | copy-start | bytes 772
  66.2 27.0 %all-to-all-start.1 = ((bf16[16,16,1440]{2,1,0:T(8,128)(2,1)}), bf16[16,16,1440]{2,1,0:T(8,128)(2,1)S(1)}, u32[]{:S(2)}, u32[]{:S(2)}) async-start(bf16[16,16,1440]{2,1,0:T(8,128)(2,1)} %fusion.9), calls=%async_computation.1 | async-start | bytes 1572864 | tf_op jit(solution)/shard_map/all_to_all | solution.py:52
where the time goes:
time: 97.3 us; the launch traced here: 96.8 us
  waiting for transfers between devices  51.1 us (53%)
  starting transfers between devices  16.8 us (17%)
  matrix products  13.3 us (14%)
  local copies, waits for them, and re-layouts  8.96 us (9%)
  other arithmetic  6.51 us (7%)
    all_to_all x1, waiting for transfers between devices, local(): lax.all_to_all(outgoing, 'ep', split_axis=0, concat_axis=0, tiled=True)  30.7 us
    all_to_all x1, waiting for transfers between devices, local(): lax.all_to_all(reduced, 'ep', split_axis=0, concat_axis=0, tiled=True)  18.5 us
    dot_general x1, matrix products, expert_half(): jnp.dot(hidden, w_down, preferred_element_type=jnp.float32)  9.4 us
    all_to_all x1, starting transfers between devices, local(): lax.all_to_all(reduced, 'ep', split_axis=0, concat_axis=0, tiled=True)  8.37 us
    all_to_all x1, starting transfers between devices, local(): lax.all_to_all(outgoing, 'ep', split_axis=0, concat_axis=0, tiled=True)  7.39 us
    dynamic_slice x1, other arithmetic, local(): given_half = lax.dynamic_index_in_dim(halves, 1 - parity, 2, keepdims=False)  3.64 us
    dot_general x1, matrix products, expert_half(): gate_part = jnp.dot(expert_rows, w_gate, preferred_element_type=jnp.float32)  3.53 us
  transfers between devices with their start and end apart: 3, of which 3 were waited for; matrix products, arithmetic and copies ran while one was open for 0% of the time, Pallas kernels for 0%

commit v1 on v0

--- a/solution.py
+++ b/solution.py
@@ -1,6 +1,10 @@
+import functools
+
 import jax
 import jax.numpy as jnp
 from jax import lax
+from jax.experimental import pallas as pl
+from jax.experimental.pallas import tpu as pltpu
 from jax.sharding import PartitionSpec as P
 
 
@@ -60,6 +64,246 @@
     return mixed.astype(jnp.bfloat16)
 
 
+def ordered_offsets(count):
+    return sorted(range(1, count), key=lambda off: (-min(off, count - off), off)) + [0]
+
+
+def column_cuts(width, step):
+    return [(low, min(low + step, width)) for low in range(0, width, step)]
+
+
+def dense_kernel(
+    slow, fast, tokens, routes, gates, w_gate, w_up, w_down, out,
+    gathered, vm_gate, vm_up, vm_down, partial, from_core, to_fast, from_fast, to_slow, from_slow,
+    w_sem, ag_send, ag_recv, core_send, core_recv, fast_send, fast_recv, slow_send, slow_recv,
+    pass_send, pass_recv, give_send, give_recv,
+):
+    rows, width = tokens.shape
+    top = routes.shape[1]
+    padded = gathered.shape[1]
+    hidden_count = vm_gate.shape[1]
+    offsets = ordered_offsets(slow)
+    device = lax.axis_index("ep")
+    core = lax.rem(device, 2)
+    chip = device // 2
+    at_slow = chip // fast
+    at_fast = lax.rem(chip, fast)
+
+    weights = [
+        pltpu.make_async_copy(source.at[0], target, w_sem.at[i])
+        for i, (source, target) in enumerate(((w_gate, vm_gate), (w_up, vm_up), (w_down, vm_down)))
+    ]
+    for copy in weights:
+        copy.start()
+
+    def name(s, f, c):
+        return {"ep": (s * fast + f) * 2 + c}
+
+    def slow_at(off):
+        return lax.rem(at_slow + off, slow)
+
+    def fast_at(off):
+        return lax.rem(at_fast + off, fast)
+
+    def block(s, f, c):
+        start = ((s * 2 + c) * fast + f) * rows
+        return pl.ds(pl.multiple_of(start, rows), rows)
+
+    def send(source, target, send_sem, recv_sem, device_id):
+        return pltpu.make_async_remote_copy(
+            src_ref=source, dst_ref=target, send_sem=send_sem, recv_sem=recv_sem,
+            device_id=device_id, device_id_type=pl.DeviceIdType.MESH,
+        )
+
+    peers = [name(slow_at(off), at_fast, core) for off in range(1, slow)]
+    peers += [name(at_slow, fast_at(off), core) for off in range(1, fast)]
+    peers += [name(at_slow, at_fast, 1 - core)]
+    barrier = pltpu.get_barrier_semaphore()
+    for peer in peers:
+        pl.semaphore_signal(barrier, inc=1, device_id=peer, device_id_type=pl.DeviceIdType.MESH)
+
+    mine = block(at_slow, at_fast, core)
+    edge = width // 128 * 128
+    lanes = lax.broadcasted_iota(jnp.int32, (rows, padded - edge), 1) + edge
+    gathered[mine, edge:] = jnp.zeros((rows, padded - edge), jnp.bfloat16)
+    gathered[mine, :width] = tokens[...]
+    scale = gates[...].astype(jnp.float32) / 65536.0
+    high = scale.astype(jnp.bfloat16).astype(jnp.float32)
+    low = scale - high
+    ids = routes[...].astype(jnp.float32)
+    tail = gathered[mine, edge:].astype(jnp.float32)
+    for k in range(top):
+        tail = jnp.where(lanes == width + k, ids[:, k : k + 1], tail)
+        tail = jnp.where(lanes == width + top + k, high[:, k : k + 1], tail)
+        tail = jnp.where(lanes == width + 2 * top + k, low[:, k : k + 1], tail)
+    gathered[mine, edge:] = tail.astype(jnp.bfloat16)
+
+    pl.semaphore_wait(barrier, len(peers))
+
+    started = []
+
+    def launch(copy):
+        copy.start()
+        started.append(copy)
+
+    def to_partner(s, f, slot):
+        where = gathered.at[block(s, f, core)]
+        launch(send(where, where, core_send.at[slot], core_recv.at[slot], name(at_slow, at_fast, 1 - core)))
+
+    def along_fast(s, step):
+        where = gathered.at[block(s, at_fast, core)]
+        for off in range(1, fast):
+            launch(send(where, where, fast_send.at[step, off], fast_recv.at[step, off], name(at_slow, fast_at(off), core)))
+
+    here = gathered.at[mine]
+    along_fast(at_slow, slow - 1)
+    for step, off in enumerate(offsets[:-1]):
+        launch(send(here, here, ag_send.at[step], ag_recv.at[step], name(slow_at(off), at_fast, core)))
+    to_partner(at_slow, at_fast, 0)
+
+    slot = 1
+    for step, off in enumerate(offsets):
+        if off:
+            s = slow_at(slow - off)
+            got = gathered.at[block(s, at_fast, core)]
+            send(got, got, ag_send.at[step], ag_recv.at[step], name(s, at_fast, core)).wait_recv()
+            along_fast(s, step)
+            to_partner(s, at_fast, slot)
+            slot += 1
+    for step in [slow - 1] + list(range(slow - 1)):
+        s = slow_at(slow - offsets[step])
+        for off in range(1, fast):
+            f = fast_at(fast - off)
+            got = gathered.at[block(s, f, core)]
+            send(got, got, fast_send.at[step, off], fast_recv.at[step, off], name(at_slow, f, core)).wait_recv()
+            to_partner(s, f, slot)
+            slot += 1
+    slot = 0
+    arrivals = [(at_slow, at_fast)] + [(slow_at(slow - off), at_fast) for off in offsets[:-1]]
+    for step in [slow - 1] + list(range(slow - 1)):
+        arrivals += [(slow_at(slow - offsets[step]), fast_at(fast - off)) for off in range(1, fast)]
+    for slot, (s, f) in enumerate(arrivals):
+        got = gathered.at[block(s, f, 1 - core)]
+        send(got, got, core_send.at[slot], core_recv.at[slot], name(at_slow, at_fast, 1 - core)).wait_recv()
+
+    weights[0].wait()
+    weights[1].wait()
+    expert = chip.astype(jnp.float32)
+    info = gathered[:, edge:].astype(jnp.float32)
+    factor = jnp.zeros((info.shape[0], 1), jnp.float32)
+    for k in range(top):
+        col = width - edge + k
+        value = info[:, col + top : col + top + 1] + info[:, col + 2 * top : col + 2 * top + 1]
+        factor += jnp.where(info[:, col : col + 1] == expert, value, 0.0)
+    x = gathered[:, :width]
+    pieces = []
+    for low_col, high_col in column_cuts(hidden_count, 256):
+        g = jnp.dot(x, vm_gate[:, low_col:high_col], preferred_element_type=jnp.float32)
+        u = jnp.dot(x, vm_up[:, low_col:high_col], preferred_element_type=jnp.float32)
+        pieces.append((jax.nn.silu(g) * u).astype(jnp.bfloat16))
+    hidden = jnp.concatenate(pieces, axis=1)
+    weights[2].wait()
+    for low_col, high_col in column_cuts(width, 512):
+        y = jnp.dot(hidden, vm_down[:, low_col:high_col], preferred_element_type=jnp.float32)
+        partial[:, low_col:high_col] = (y * factor).astype(jnp.bfloat16)
+
+    def pair(s, c):
+        return pl.ds(pl.multiple_of((s * 2 + c) * fast * rows, rows), fast * rows)
+
+    def tile(index):
+        return pl.ds(pl.multiple_of(index * rows, rows), rows)
+
+    def core_copy(step):
+        s = slow_at(offsets[step])
+        return send(
+            partial.at[pair(s, 1 - core)], from_core.at[pl.ds(step * fast * rows, fast * rows)],
+            pass_send.at[step], pass_recv.at[step], name(at_slow, at_fast, 1 - core),
+        )
+
+    def both_cores(step, f):
+        s = slow_at(offsets[step])
+        mine_part = partial[block(s, f, core), :].astype(jnp.float32)
+        return mine_part + from_core[tile(step * fast + f), :].astype(jnp.float32)
+
+    def fast_copy(step, off):
+        place = pl.ds((step * (fast - 1) + off - 1) * rows, rows)
+        return send(
+            to_fast.at[place], from_fast.at[place],
+            give_send.at[step, off], give_recv.at[step, off], name(at_slow, fast_at(off), core),
+        )
+
+    def slow_copy(step):
+        place = pl.ds(step * rows, rows)
+        return send(
+            to_slow.at[place], from_slow.at[place],
+            slow_send.at[step], slow_recv.at[step], name(slow_at(offsets[step]), at_fast, core),
+        )
+
+    for step in range(slow):
+        launch(core_copy(step))
+    for step in range(slow):
+        core_copy(step).wait_recv()
+        for off in range(1, fast):
+            place = (step * (fast - 1) + off - 1) * rows
+            to_fast[place : place + rows, :] = both_cores(step, fast_at(off)).astype(jnp.bfloat16)
+            launch(fast_copy(step, off))
+    for step in range(slow):
+        total = both_cores(step, at_fast)
+        for off in range(1, fast):
+            fast_copy(step, off).wait_recv()
+            place = (step * (fast - 1) + off - 1) * rows
+            total += from_fast[place : place + rows, :].astype(jnp.float32)
+        if offsets[step]:
+            to_slow[step * rows : (step + 1) * rows, :] = total.astype(jnp.bfloat16)
+            launch(slow_copy(step))
+    for step in range(slow - 1):
+        slow_copy(step).wait_recv()
+        total += from_slow[step * rows : (step + 1) * rows, :].astype(jnp.float32)
+    out[...] = total.astype(out.dtype)
+    for copy in started:
+        copy.wait_send()
+
+
+def dense_local(slow, fast, tokens, routes, gate_fixed, gate_weight, up_weight, down_weight):
+    rows, width = tokens.shape
+    top = routes.shape[1]
+    hidden_count = gate_weight.shape[2]
+    padded = -(-(width + 3 * top) // 128) * 128
+    every = slow * fast * 2 * rows
+    dma = pltpu.SemaphoreType.DMA
+    half = slow * fast * rows
+    vmem = pl.BlockSpec(memory_space=pltpu.VMEM)
+    anywhere = pl.BlockSpec(memory_space=pl.ANY)
+    return pl.pallas_call(
+        functools.partial(dense_kernel, slow, fast),
+        out_shape=jax.ShapeDtypeStruct((rows, width), jnp.bfloat16),
+        in_specs=[vmem, vmem, vmem, anywhere, anywhere, anywhere],
+        out_specs=vmem,
+        scratch_shapes=[
+            pltpu.VMEM((every, padded), jnp.bfloat16),
+            pltpu.VMEM(gate_weight.shape[1:], jnp.bfloat16),
+            pltpu.VMEM(up_weight.shape[1:], jnp.bfloat16),
+            pltpu.VMEM(down_weight.shape[1:], jnp.bfloat16),
+            pltpu.VMEM((every, width), jnp.bfloat16),
+            pltpu.VMEM((half, width), jnp.bfloat16),
+            pltpu.VMEM((slow * (fast - 1) * rows, width), jnp.bfloat16),
+            pltpu.VMEM((slow * (fast - 1) * rows, width), jnp.bfloat16),
+            pltpu.VMEM(((slow - 1) * rows, width), jnp.bfloat16),
+            pltpu.VMEM(((slow - 1) * rows, width), jnp.bfloat16),
+            dma((3,)),
+            dma((slow,)), dma((slow,)),
+            dma((slow * fast,)), dma((slow * fast,)),
+            dma((slow, fast)), dma((slow, fast)),
+            dma((slow,)), dma((slow,)),
+            dma((slow,)), dma((slow,)),
+            dma((slow, fast)), dma((slow, fast)),
+        ],
+        compiler_params=pltpu.CompilerParams(
+            collective_id=0, has_side_effects=True, vmem_limit_bytes=60 * 2**20
+        ),
+    )(tokens, routes, gate_fixed, gate_weight, up_weight, down_weight)
+
+
 def solution(mesh):
     placed = (
         P(("groups", "ep"), None),
@@ -69,6 +313,14 @@
         P("ep", None, None),
         P("ep", None, None),
     )
+    chips = mesh.shape["ep"] // 2
+
+    def body(*args):
+        top = args[1].shape[1]
+        if chips <= 4 * top and chips % 4 == 0:
+            return dense_local(4, chips // 4, *args)
+        return local(*args)
+
     return jax.shard_map(
-        local, mesh=mesh, in_specs=placed, out_specs=P(("groups", "ep"), None), check_vma=False
-    )
+        body, mesh=mesh, in_specs=placed, out_specs=P(("groups", "ep"), None), check_vma=False
+    )

time: 97.3 us -> 56.7 us (0.58)
  waiting for transfers between devices: 51.1 us -> 0 us
  Pallas kernels: 0 us -> 38.9 us
  starting transfers between devices: 16.8 us -> 0 us
  matrix products: 13.3 us -> 0 us
  local copies, waits for them, and re-layouts: 8.96 us -> 17.3 us
  other arithmetic: 6.51 us -> 0 us
    all_to_all x2 -> x0, waiting for transfers between devices: 49.1 us -> none  [the longest x1 30.7 us: local(): lax.all_to_all(outgoing, 'ep', split_axis=0, concat_axis=0, tiled=True)]
    pallas_call x0 -> x1, Pallas kernels: none -> 38.9 us  [dense_local(): pl.pallas_call(functools.partial(dense_kernel, slow, fast), out_shape=jax...]
    unnamed x6 -> x5, local copies, waits for them, and re-layouts: 0.93 us -> 17.3 us
    all_to_all x2 -> x0, starting transfers between devices: 15.8 us -> none  [the longest x1 8.37 us: local(): lax.all_to_all(reduced, 'ep', split_axis=0, concat_axis=0, tiled=True)]
    dot_general x3 -> x0, matrix products: 13.3 us -> none  [the longest x1 9.4 us: expert_half(): jnp.dot(hidden, w_down, preferred_element_type=jnp.float32)]
    dynamic_slice x1 -> x0, other arithmetic: 3.64 us -> none  [local(): given_half = lax.dynamic_index_in_dim(halves, 1 - parity, 2, keepdims=False)]
    convert_element_type x2 -> x0, local copies, waits for them, and re-layouts: 2.19 us -> none  [the longest x1 1.82 us: expert_half(): jnp.dot(hidden, w_down, preferred_element_type=jnp.float32)]
    another operation x1 -> x0, local copies, waits for them, and re-layouts: 1.92 us -> none  [local(): halves = partial_value.reshape(devices_ep, capacity, 2, width // 2)]
  transfers between devices with their start and end apart: 3 -> 0, of which waited for: 3 -> 0; matrix products, arithmetic and copies ran while one was open for 0% -> 0% of each run, Pallas kernels for 0% -> 0%
where the time goes in v1:
time: 56.7 us; the launch traced here: 56.2 us
  Pallas kernels  38.9 us (69%)
  local copies, waits for them, and re-layouts  17.3 us (31%)
    pallas_call x1, Pallas kernels, dense_local(): pl.pallas_call(functools.partial(dense_kernel, slow, fast), out_shape=jax...  38.9 us
    unnamed x5, local copies, waits for them, and re-layouts  17.3 us

profile of v1, /device:TPU:0, one launch (start us, length us, event | category | flops | bytes accessed | tf_op | source)
XLA Modules:
  0.0 56.2 jit_solution(16102258766983778314)
XLA Ops:
  0.0 1.4 %copy.7.routes = s32[16,4]{1,0:T(8,128)} copy(s32[16,4]{0,1:T(4,128)} %param.7) | data formatting | bytes 512 | tf_op args[1]
  1.4 1.3 %copy.8.gates = s32[16,4]{1,0:T(8,128)} copy(s32[16,4]{0,1:T(4,128)} %param.8) | data formatting | bytes 512 | tf_op args[2]
  2.7 6.5 %copy.9.w_gate = bf16[1,2880,720]{2,1,0:T(8,128)(2,1)} copy(bf16[1,2880,720]{1,2,0:T(8,128)(2,1)} %param.9) | data formatting | bytes 8294400 | tf_op args[3]
  9.2 6.5 %copy.10.w_up = bf16[1,2880,720]{2,1,0:T(8,128)(2,1)} copy(bf16[1,2880,720]{1,2,0:T(8,128)(2,1)} %param.10) | data formatting | bytes 8294400 | tf_op args[4]
  15.7 38.9 %shard_map.64 = bf16[16,2880]{1,0:T(8,128)(2,1)} custom-call(bf16[16,2880]{1,0:T(8,128)(2,1)} %tokens.1, s32[16,4]{1,0:T(8,128)} %copy.7.routes, s32[16,4]{1,0:T(8,128)} %copy.8.gates, bf16[1,2880,720]{2,1,0:T(8,128)(2,1)} %copy.9.w_gate, bf16[1,2880,720]{2,1,0:T(8,128)(2,1)} %copy.10.w_up, bf16[1,720,2880]{2,1,0:T(8,128)(2,1)} %w_down.1), custom_call_target="tpu_custom_call" | custom-call | tf_op jit(solution)/shard_map/pallas_call | solution.py:277
  54.7 1.5 %copy.12 = bf16[16,2880]{1,0:T(8,128)(2,1)} copy(bf16[16,2880]{1,0:T(8,128)(2,1)} %shard_map.64) | data formatting | bytes 184320

commit v2 on v1

--- a/solution.py
+++ b/solution.py
@@ -64,6 +64,9 @@
     return mixed.astype(jnp.bfloat16)
 
 
+NT = (((1,), (1,)), ((), ()))
+
+
 def ordered_offsets(count):
     return sorted(range(1, count), key=lambda off: (-min(off, count - off), off)) + [0]
 
@@ -79,9 +82,9 @@
     pass_send, pass_recv, give_send, give_recv,
 ):
     rows, width = tokens.shape
-    top = routes.shape[1]
+    top = routes.shape[0]
     padded = gathered.shape[1]
-    hidden_count = vm_gate.shape[1]
+    hidden_count = vm_gate.shape[0]
     offsets = ordered_offsets(slow)
     device = lax.axis_index("ep")
     core = lax.rem(device, 2)
@@ -127,10 +130,10 @@
     lanes = lax.broadcasted_iota(jnp.int32, (rows, padded - edge), 1) + edge
     gathered[mine, edge:] = jnp.zeros((rows, padded - edge), jnp.bfloat16)
     gathered[mine, :width] = tokens[...]
-    scale = gates[...].astype(jnp.float32) / 65536.0
+    scale = jnp.transpose(gates[...].astype(jnp.float32)) / 65536.0
     high = scale.astype(jnp.bfloat16).astype(jnp.float32)
     low = scale - high
-    ids = routes[...].astype(jnp.float32)
+    ids = jnp.transpose(routes[...].astype(jnp.float32))
     tail = gathered[mine, edge:].astype(jnp.float32)
     for k in range(top):
         tail = jnp.where(lanes == width + k, ids[:, k : k + 1], tail)
@@ -159,53 +162,65 @@
     along_fast(at_slow, slow - 1)
     for step, off in enumerate(offsets[:-1]):
         launch(send(here, here, ag_send.at[step], ag_recv.at[step], name(slow_at(off), at_fast, core)))
-    to_partner(at_slow, at_fast, 0)
-
-    slot = 1
-    for step, off in enumerate(offsets):
-        if off:
-            s = slow_at(slow - off)
-            got = gathered.at[block(s, at_fast, core)]
-            send(got, got, ag_send.at[step], ag_recv.at[step], name(s, at_fast, core)).wait_recv()
-            along_fast(s, step)
-            to_partner(s, at_fast, slot)
-            slot += 1
-    for step in [slow - 1] + list(range(slow - 1)):
-        s = slow_at(slow - offsets[step])
+    to_partner(at_slow, at_fast, (slow - 1) * fast)
+
+    own = slow - 1
+    order = [own] + list(range(own))
+    chunk_rows = 2 * fast * rows
+
+    def source(step):
+        return slow_at(slow - offsets[step])
+
+    def take_slow(step):
+        if step == own:
+            return
+        s = source(step)
+        got = gathered.at[block(s, at_fast, core)]
+        send(got, got, ag_send.at[step], ag_recv.at[step], name(s, at_fast, core)).wait_recv()
+        along_fast(s, step)
+        to_partner(s, at_fast, step * fast)
+
+    def take_fast(step):
         for off in range(1, fast):
             f = fast_at(fast - off)
-            got = gathered.at[block(s, f, core)]
+            got = gathered.at[block(source(step), f, core)]
             send(got, got, fast_send.at[step, off], fast_recv.at[step, off], name(at_slow, f, core)).wait_recv()
-            to_partner(s, f, slot)
-            slot += 1
-    slot = 0
-    arrivals = [(at_slow, at_fast)] + [(slow_at(slow - off), at_fast) for off in offsets[:-1]]
-    for step in [slow - 1] + list(range(slow - 1)):
-        arrivals += [(slow_at(slow - offsets[step]), fast_at(fast - off)) for off in range(1, fast)]
-    for slot, (s, f) in enumerate(arrivals):
-        got = gathered.at[block(s, f, 1 - core)]
-        send(got, got, core_send.at[slot], core_recv.at[slot], name(at_slow, at_fast, 1 - core)).wait_recv()
-
-    weights[0].wait()
-    weights[1].wait()
-    expert = chip.astype(jnp.float32)
-    info = gathered[:, edge:].astype(jnp.float32)
-    factor = jnp.zeros((info.shape[0], 1), jnp.float32)
-    for k in range(top):
-        col = width - edge + k
-        value = info[:, col + top : col + top + 1] + info[:, col + 2 * top : col + 2 * top + 1]
-        factor += jnp.where(info[:, col : col + 1] == expert, value, 0.0)
-    x = gathered[:, :width]
-    pieces = []
-    for low_col, high_col in column_cuts(hidden_count, 256):
-        g = jnp.dot(x, vm_gate[:, low_col:high_col], preferred_element_type=jnp.float32)
-        u = jnp.dot(x, vm_up[:, low_col:high_col], preferred_element_type=jnp.float32)
-        pieces.append((jax.nn.silu(g) * u).astype(jnp.bfloat16))
-    hidden = jnp.concatenate(pieces, axis=1)
-    weights[2].wait()
-    for low_col, high_col in column_cuts(width, 512):
-        y = jnp.dot(hidden, vm_down[:, low_col:high_col], preferred_element_type=jnp.float32)
-        partial[:, low_col:high_col] = (y * factor).astype(jnp.bfloat16)
+            to_partner(source(step), f, step * fast + off)
+
+    def take_core(step):
+        for off in range(fast):
+            slot = step * fast + off
+            got = gathered.at[block(source(step), fast_at(fast - off), 1 - core)]
+            send(got, got, core_send.at[slot], core_recv.at[slot], name(at_slow, at_fast, 1 - core)).wait_recv()
+
+    def chunk(step):
+        return pl.ds(pl.multiple_of(source(step) * chunk_rows, chunk_rows), chunk_rows)
+
+    def half_expert(steps):
+        expert = chip.astype(jnp.float32)
+        factors = []
+        for step in steps:
+            info = gathered[chunk(step), edge:].astype(jnp.float32)
+            factor = jnp.zeros((chunk_rows, 1), jnp.float32)
+            for k in range(top):
+                col = width - edge + k
+                value = info[:, col + top : col + top + 1] + info[:, col + 2 * top : col + 2 * top + 1]
+                factor += jnp.where(info[:, col : col + 1] == expert, value, 0.0)
+            factors.append(factor)
+        x = jnp.concatenate([gathered[chunk(step), :width] for step in steps], axis=0)
+        pieces = []
+        for low_col, high_col in column_cuts(hidden_count, 256):
+            g = lax.dot_general(x, vm_gate[low_col:high_col, :], NT, preferred_element_type=jnp.float32)
+            u = lax.dot_general(x, vm_up[low_col:high_col, :], NT, preferred_element_type=jnp.float32)
+            pieces.append((jax.nn.silu(g) * u).astype(jnp.bfloat16))
+        hidden = jnp.concatenate(pieces, axis=1)
+        if steps[0] == own:
+            weights[2].wait()
+        for low_col, high_col in column_cuts(width, 512):
+            y = jnp.dot(hidden, vm_down[:, low_col:high_col], preferred_element_type=jnp.float32)
+            for i, step in enumerate(steps):
+                part = y[i * chunk_rows : (i + 1) * chunk_rows] * factors[i]
+                partial[chunk(step), low_col:high_col] = part.astype(jnp.bfloat16)
 
     def pair(s, c):
         return pl.ds(pl.multiple_of((s * 2 + c) * fast * rows, rows), fast * rows)
@@ -214,14 +229,14 @@
         return pl.ds(pl.multiple_of(index * rows, rows), rows)
 
     def core_copy(step):
-        s = slow_at(offsets[step])
+        s = source(step)
         return send(
             partial.at[pair(s, 1 - core)], from_core.at[pl.ds(step * fast * rows, fast * rows)],
             pass_send.at[step], pass_recv.at[step], name(at_slow, at_fast, 1 - core),
         )
 
     def both_cores(step, f):
-        s = slow_at(offsets[step])
+        s = source(step)
         mine_part = partial[block(s, f, core), :].astype(jnp.float32)
         return mine_part + from_core[tile(step * fast + f), :].astype(jnp.float32)
 
@@ -236,17 +251,42 @@
         place = pl.ds(step * rows, rows)
         return send(
             to_slow.at[place], from_slow.at[place],
-            slow_send.at[step], slow_recv.at[step], name(slow_at(offsets[step]), at_fast, core),
+            slow_send.at[step], slow_recv.at[step], name(source(step), at_fast, core),
         )
 
-    for step in range(slow):
-        launch(core_copy(step))
-    for step in range(slow):
+    def give_fast(step):
         core_copy(step).wait_recv()
         for off in range(1, fast):
             place = (step * (fast - 1) + off - 1) * rows
             to_fast[place : place + rows, :] = both_cores(step, fast_at(off)).astype(jnp.bfloat16)
             launch(fast_copy(step, off))
+
+    first, second = order[: slow // 2], order[slow // 2 :]
+    for step in first:
+        take_slow(step)
+    for step in first:
+        take_fast(step)
+    for step in second[:-1]:
+        take_slow(step)
+    for step in first:
+        take_core(step)
+    weights[0].wait()
+    weights[1].wait()
+    half_expert(first)
+    for step in first[1:] + first[:1]:
+        launch(core_copy(step))
+    take_slow(second[-1])
+    for step in second:
+        take_fast(step)
+    for step in first[1:] + first[:1]:
+        give_fast(step)
+    for step in second:
+        take_core(step)
+    half_expert(second)
+    for step in second:
+        launch(core_copy(step))
+    for step in second:
+        give_fast(step)
     for step in range(slow):
         total = both_cores(step, at_fast)
         for off in range(1, fast):
@@ -267,7 +307,8 @@
 def dense_local(slow, fast, tokens, routes, gate_fixed, gate_weight, up_weight, down_weight):
     rows, width = tokens.shape
     top = routes.shape[1]
-    hidden_count = gate_weight.shape[2]
+    gate_weight = jnp.swapaxes(gate_weight, 1, 2)
+    up_weight = jnp.swapaxes(up_weight, 1, 2)
     padded = -(-(width + 3 * top) // 128) * 128
     every = slow * fast * 2 * rows
     dma = pltpu.SemaphoreType.DMA
@@ -301,7 +342,7 @@
         compiler_params=pltpu.CompilerParams(
             collective_id=0, has_side_effects=True, vmem_limit_bytes=60 * 2**20
         ),
-    )(tokens, routes, gate_fixed, gate_weight, up_weight, down_weight)
+    )(tokens, routes.T, gate_fixed.T, gate_weight, up_weight, down_weight)
 
 
 def solution(mesh):

time: 56.7 us -> 46 us (0.81)
  local copies, waits for them, and re-layouts: 17.3 us -> 1.54 us
  Pallas kernels: 38.9 us -> 44.3 us
    unnamed x5 -> x1, local copies, waits for them, and re-layouts: 17.3 us -> 1.54 us
    pallas_call x1, Pallas kernels: 38.9 us -> 44.3 us  [dense_local(): pl.pallas_call(functools.partial(dense_kernel, slow, fast), out_shape=jax...]
where the time goes in v2:
time: 46 us; the launch traced here: 45.9 us
  Pallas kernels  44.3 us (96%)
  local copies, waits for them, and re-layouts  1.54 us (3%)
    pallas_call x1, Pallas kernels, dense_local(): pl.pallas_call(functools.partial(dense_kernel, slow, fast), out_shape=jax...  44.3 us
    unnamed x1, local copies, waits for them, and re-layouts  1.54 us

profile of v2, /device:TPU:0, one launch (start us, length us, event | category | flops | bytes accessed | tf_op | source)
XLA Modules:
  0.0 45.9 jit_solution(6432711604094898467)
XLA Ops:
  0.0 44.3 %shard_map.64 = bf16[16,2880]{1,0:T(8,128)(2,1)} custom-call(bf16[16,2880]{1,0:T(8,128)(2,1)} %tokens.1, s32[4,16]{1,0:T(4,128)} %bitcast.6, s32[4,16]{1,0:T(4,128)} %bitcast.7, bf16[1,720,2880]{2,1,0:T(8,128)(2,1)} %bitcast.4, bf16[1,720,2880]{2,1,0:T(8,128)(2,1)} %bitcast.5, bf16[1,720,2880]{2,1,0:T(8,128)(2,1)} %w_down.1), custom_call_target="tpu_custom_call" | custom-call | tf_op jit(solution)/shard_map/pallas_call | solution.py:318
  44.3 1.5 %copy.8 = bf16[16,2880]{1,0:T(8,128)(2,1)} copy(bf16[16,2880]{1,0:T(8,128)(2,1)} %shard_map.64) | data formatting | bytes 184320

commit v3 on v2

--- a/solution.py
+++ b/solution.py
@@ -67,10 +67,6 @@
 NT = (((1,), (1,)), ((), ()))
 
 
-def ordered_offsets(count):
-    return sorted(range(1, count), key=lambda off: (-min(off, count - off), off)) + [0]
-
-
 def column_cuts(width, step):
     return [(low, min(low + step, width)) for low in range(0, width, step)]
 
@@ -85,7 +81,6 @@
     top = routes.shape[0]
     padded = gathered.shape[1]
     hidden_count = vm_gate.shape[0]
-    offsets = ordered_offsets(slow)
     device = lax.axis_index("ep")
     core = lax.rem(device, 2)
     chip = device // 2
@@ -160,8 +155,19 @@
 
     here = gathered.at[mine]
     along_fast(at_slow, slow - 1)
-    for step, off in enumerate(offsets[:-1]):
-        launch(send(here, here, ag_send.at[step], ag_recv.at[step], name(slow_at(off), at_fast, core)))
+    outward, across = at_slow + 1 - 2 * lax.rem(at_slow, 2), slow - 1 - at_slow
+    inner = (at_slow % 3) != 0
+
+    def to_slow_chip(s, place, sem, slot):
+        where = gathered.at[block(s, at_fast, core)]
+        return send(where, where, ag_send.at[sem], ag_recv.at[slot], name(place, at_fast, core))
+
+    to_slow_chip(at_slow, outward, 0, 0).start()
+
+    @pl.when(inner)
+    def _():
+        to_slow_chip(at_slow, across, 1, 1).start()
+
     to_partner(at_slow, at_fast, (slow - 1) * fast)
 
     own = slow - 1
@@ -169,14 +175,22 @@
     chunk_rows = 2 * fast * rows
 
     def source(step):
-        return slow_at(slow - offsets[step])
+        return [outward, 2 - at_slow // 2, 3 - 3 * (at_slow // 2), at_slow][step]
 
     def take_slow(step):
         if step == own:
             return
         s = source(step)
         got = gathered.at[block(s, at_fast, core)]
-        send(got, got, ag_send.at[step], ag_recv.at[step], name(s, at_fast, core)).wait_recv()
+        send(got, got, ag_send.at[step], ag_recv.at[step], name(outward, at_fast, core)).wait_recv()
+
+        @pl.when(inner)
+        def _():
+            if step == 0:
+                to_slow_chip(s, across, 2, 2).start()
+            else:
+                to_slow_chip(s, outward, 2 + step, step).start()
+
         along_fast(s, step)
         to_partner(s, at_fast, step * fast)
 
@@ -248,10 +262,9 @@
         )
 
     def slow_copy(step):
-        place = pl.ds(step * rows, rows)
         return send(
-            to_slow.at[place], from_slow.at[place],
-            slow_send.at[step], slow_recv.at[step], name(source(step), at_fast, core),
+            to_slow.at[pl.ds(step * rows, rows)], from_slow.at[tile(at_slow)],
+            slow_send.at[step], slow_recv.at[at_slow], name(source(step), at_fast, core),
         )
 
     def give_fast(step):
@@ -262,12 +275,12 @@
             launch(fast_copy(step, off))
 
     first, second = order[: slow // 2], order[slow // 2 :]
-    for step in first:
-        take_slow(step)
-    for step in first:
-        take_fast(step)
-    for step in second[:-1]:
-        take_slow(step)
+    take_slow(0)
+    take_slow(1)
+    take_fast(own)
+    take_fast(0)
+    take_slow(2)
+    take_fast(1)
     for step in first:
         take_core(step)
     weights[0].wait()
@@ -275,9 +288,7 @@
     half_expert(first)
     for step in first[1:] + first[:1]:
         launch(core_copy(step))
-    take_slow(second[-1])
-    for step in second:
-        take_fast(step)
+    take_fast(2)
     for step in first[1:] + first[:1]:
         give_fast(step)
     for step in second:
@@ -293,15 +304,23 @@
             fast_copy(step, off).wait_recv()
             place = (step * (fast - 1) + off - 1) * rows
             total += from_fast[place : place + rows, :].astype(jnp.float32)
-        if offsets[step]:
+        if step != own:
             to_slow[step * rows : (step + 1) * rows, :] = total.astype(jnp.bfloat16)
             launch(slow_copy(step))
-    for step in range(slow - 1):
-        slow_copy(step).wait_recv()
-        total += from_slow[step * rows : (step + 1) * rows, :].astype(jnp.float32)
+    for off in range(1, slow):
+        s = slow_at(off)
+        got = from_slow.at[tile(s)]
+        send(got, got, slow_send.at[0], slow_recv.at[s], name(s, at_fast, core)).wait_recv()
+        total += from_slow[tile(s), :].astype(jnp.float32)
     out[...] = total.astype(out.dtype)
     for copy in started:
         copy.wait_send()
+    to_slow_chip(at_slow, outward, 0, 0).wait_send()
+
+    @pl.when(inner)
+    def _():
+        for sem in range(1, 5):
+            to_slow_chip(at_slow, outward, sem, 0).wait_send()
 
 
 def dense_local(slow, fast, tokens, routes, gate_fixed, gate_weight, up_weight, down_weight):
@@ -330,9 +349,9 @@
             pltpu.VMEM((slow * (fast - 1) * rows, width), jnp.bfloat16),
             pltpu.VMEM((slow * (fast - 1) * rows, width), jnp.bfloat16),
             pltpu.VMEM(((slow - 1) * rows, width), jnp.bfloat16),
-            pltpu.VMEM(((slow - 1) * rows, width), jnp.bfloat16),
+            pltpu.VMEM((slow * rows, width), jnp.bfloat16),
             dma((3,)),
-            dma((slow,)), dma((slow,)),
+            dma((5,)), dma((3,)),
             dma((slow * fast,)), dma((slow * fast,)),
             dma((slow, fast)), dma((slow, fast)),
             dma((slow,)), dma((slow,)),

time: 46 us -> 41.4 us (0.900)
  Pallas kernels: 44.3 us -> 39.7 us
    pallas_call x1, Pallas kernels: 44.3 us -> 39.7 us  [dense_local(): pl.pallas_call(functools.partial(dense_kernel, slow, fast), out_shape=jax...]
where the time goes in v3:
time: 41.4 us; the launch traced here: 41.2 us
  Pallas kernels  39.7 us (96%)
  local copies, waits for them, and re-layouts  1.54 us (4%)
    pallas_call x1, Pallas kernels, dense_local(): pl.pallas_call(functools.partial(dense_kernel, slow, fast), out_shape=jax...  39.7 us
    unnamed x1, local copies, waits for them, and re-layouts  1.54 us

profile of v3, /device:TPU:0, one launch (start us, length us, event | category | flops | bytes accessed | tf_op | source)
XLA Modules:
  0.0 41.2 jit_solution(9607908180893944863)
XLA Ops:
  0.0 39.7 %shard_map.64 = bf16[16,2880]{1,0:T(8,128)(2,1)} custom-call(bf16[16,2880]{1,0:T(8,128)(2,1)} %tokens.1, s32[4,16]{1,0:T(4,128)} %bitcast.6, s32[4,16]{1,0:T(4,128)} %bitcast.7, bf16[1,720,2880]{2,1,0:T(8,128)(2,1)} %bitcast.4, bf16[1,720,2880]{2,1,0:T(8,128)(2,1)} %bitcast.5, bf16[1,720,2880]{2,1,0:T(8,128)(2,1)} %w_down.1), custom_call_target="tpu_custom_call" | custom-call | tf_op jit(solution)/shard_map/pallas_call | solution.py:337
  39.7 1.5 %copy.8 = bf16[16,2880]{1,0:T(8,128)(2,1)} copy(bf16[16,2880]{1,0:T(8,128)(2,1)} %shard_map.64) | data formatting | bytes 184320

commit v4 on v3

--- a/solution.py
+++ b/solution.py
@@ -294,19 +294,26 @@
     for step in second:
         take_core(step)
     half_expert(second)
-    for step in second:
+    for step in second[::-1]:
         launch(core_copy(step))
-    for step in second:
-        give_fast(step)
-    for step in range(slow):
+
+    def finish(step):
         total = both_cores(step, at_fast)
         for off in range(1, fast):
             fast_copy(step, off).wait_recv()
             place = (step * (fast - 1) + off - 1) * rows
             total += from_fast[place : place + rows, :].astype(jnp.float32)
-        if step != own:
-            to_slow[step * rows : (step + 1) * rows, :] = total.astype(jnp.bfloat16)
-            launch(slow_copy(step))
+        if step == own:
+            return total
+        to_slow[step * rows : (step + 1) * rows, :] = total.astype(jnp.bfloat16)
+        launch(slow_copy(step))
+
+    finish(0)
+    for step in second[::-1]:
+        give_fast(step)
+    for step in second[::-1]:
+        finish(step)
+    total = finish(own)
     for off in range(1, slow):
         s = slow_at(off)
         got = from_slow.at[tile(s)]

time: 41.4 us -> 40.4 us (0.976)
  Pallas kernels: 39.7 us -> 38.7 us
    pallas_call x1, Pallas kernels: 39.7 us -> 38.7 us  [dense_local(): pl.pallas_call(functools.partial(dense_kernel, slow, fast), out_shape=jax...]
where the time goes in v4:
time: 40.4 us; the launch traced here: 40.2 us
  Pallas kernels  38.7 us (96%)
  local copies, waits for them, and re-layouts  1.54 us (4%)
    pallas_call x1, Pallas kernels, dense_local(): pl.pallas_call(functools.partial(dense_kernel, slow, fast), out_shape=jax...  38.7 us
    unnamed x1, local copies, waits for them, and re-layouts  1.54 us

profile of v4, /device:TPU:0, one launch (start us, length us, event | category | flops | bytes accessed | tf_op | source)
XLA Modules:
  0.0 40.2 jit_solution(14119719956833897195)
XLA Ops:
  0.0 38.7 %shard_map.64 = bf16[16,2880]{1,0:T(8,128)(2,1)} custom-call(bf16[16,2880]{1,0:T(8,128)(2,1)} %tokens.1, s32[4,16]{1,0:T(4,128)} %bitcast.6, s32[4,16]{1,0:T(4,128)} %bitcast.7, bf16[1,720,2880]{2,1,0:T(8,128)(2,1)} %bitcast.4, bf16[1,720,2880]{2,1,0:T(8,128)(2,1)} %bitcast.5, bf16[1,720,2880]{2,1,0:T(8,128)(2,1)} %w_down.1), custom_call_target="tpu_custom_call" | custom-call | tf_op jit(solution)/shard_map/pallas_call | solution.py:344
  38.7 1.5 %copy.8 = bf16[16,2880]{1,0:T(8,128)(2,1)} copy(bf16[16,2880]{1,0:T(8,128)(2,1)} %shard_map.64) | data formatting | bytes 184320
